TPU v7x, 128 devices: a whole 4x4x4 slice. The times are simulated.
128 devices in a mesh: depth: 2 (over core), row: 16 (over z, x), col: 4 (over y).
Axes of the slice: x: 4, y: 4, z: 4, core: 2. Of those that a mesh axis runs over, the one named last changes fastest.
Arguments:
- right_side: bfloat16 [4, 16, 8, 128, 512], P(None, 'row', ('depth', 'col')), may hold values from -6 to 6
- inverse_diag: bfloat16 [4, 16, 8, 1, 128, 128], P(None, 'row', ('depth', 'col')), may hold values from -2 to 2.5, as said below
- coupling: bfloat16 [3, 16, 1024, 8, 2048], P(None, 'row', None, ('depth', 'col')), may hold values from -0.0625 to 0.0625
- pattern: int32 [3, 16, 8, 8, 16], P(None, 'row', None, ('depth', 'col')), may hold values 0 or 1
Outputs:
- forward_solution: bfloat16 [4, 16, 8, 128, 512], P(None, 'row', ('depth', 'col'))
- solution: bfloat16 [4, 16, 8, 128, 512], P(None, 'row', ('depth', 'col'))
Inputs may be any that keep to these rules, and one draw needn't show every extreme that they name: `inverse_diag`: each block is lower triangular with positive diagonal.
All inputs are finite; a program needn't handle non-finite values. No bound on the sum of `pattern` on one device may be relied on, other than what follows from the above.
Results may differ from a plain program's by a relative error of at most 0.025.
Values may be sent and summed in bfloat16 or wider, within the bound.
A program may use at most 128 MiB of HBM per device.

v0:
```python
import jax
import jax.numpy as jnp
from jax import lax
from jax.sharding import PartitionSpec as P


def apply_inverse(inverse, vector, transposed):
    blocks_in = vector.reshape(inverse.shape[0], inverse.shape[1], vector.shape[-1])
    einsum_form = "tji,tjn->tin" if transposed else "tij,tjn->tin"
    result = jnp.einsum(einsum_form, inverse, blocks_in, preferred_element_type=jnp.float32)
    return result.astype(jnp.bfloat16).reshape(vector.shape)


def lift_upward(masked, share_in):
    portion = lax.all_gather(share_in, "row", axis=0, tiled=True)
    span_rows = portion.shape[0] * portion.shape[2]
    return jnp.dot(
        masked, portion.reshape(span_rows, portion.shape[-1]), preferred_element_type=jnp.float32
    )


def carry_downward(masked, share_in):
    portion = lax.all_gather(share_in, ("depth", "col"), axis=1, tiled=True)
    span_rows = portion.shape[1] * portion.shape[2]
    return lax.dot_general(
        masked,
        portion.reshape(span_rows, portion.shape[-1]),
        (((0,), (0,)), ((), ())),
        preferred_element_type=jnp.float32,
    )


def forward_sum(partial_value, share_rows):
    blocks = partial_value.reshape(
        lax.axis_size(("depth", "col")), share_rows, partial_value.shape[-1]
    )
    summed = lax.psum(blocks.astype(jnp.bfloat16), ("depth", "col")).astype(jnp.float32)
    return lax.dynamic_index_in_dim(summed, lax.axis_index(("depth", "col")), 0, keepdims=False)


def backward_sum(partial_value, share_rows):
    blocks = partial_value.reshape(lax.axis_size("row"), share_rows, partial_value.shape[-1])
    summed = lax.psum(blocks.astype(jnp.bfloat16), "row").astype(jnp.float32)
    return lax.dynamic_index_in_dim(summed, lax.axis_index("row"), 0, keepdims=False)


def body(right_side, inverse_diag, coupling, pattern):
    levels = right_side.shape[0]
    share_rows = right_side.shape[3]
    rhs_cols = right_side.shape[4]
    block_width = inverse_diag.shape[-1]
    masked = []
    for pair_at in range(levels - 1):
        slab = coupling[pair_at, 0, :, 0, :]
        gate = pattern[pair_at, 0, :, 0, :].astype(jnp.bfloat16)
        shaped = (
            slab.reshape(gate.shape[0], block_width, gate.shape[1], block_width)
            * gate[:, None, :, None]
        )
        masked.append(shaped.reshape(slab.shape))
    panel_spans = [(0, rhs_cols)]
    fwd_levels = []
    for level_at in range(levels):
        pieces = []
        for panel_at, (col_first, col_last) in enumerate(panel_spans):
            source = right_side[level_at, 0, 0, :, col_first:col_last]
            if level_at == 0:
                residual = source
            else:
                partial_value = lift_upward(
                    masked[level_at - 1], fwd_levels[level_at - 1][panel_at][None, None]
                )
                residual = (
                    source.astype(jnp.float32) - forward_sum(partial_value, share_rows)
                ).astype(jnp.bfloat16)
            pieces.append(apply_inverse(inverse_diag[level_at, 0, 0], residual, False))
        fwd_levels.append(pieces)
    bwd_levels = [None] * levels
    for level_at in reversed(range(levels)):
        pieces = []
        panel_at = 0
        known_part = fwd_levels[level_at][panel_at]
        if level_at == levels - 1:
            residual = known_part
        else:
            partial_value = carry_downward(
                masked[level_at], bwd_levels[level_at + 1][panel_at][None, None]
            )
            residual = (
                known_part.astype(jnp.float32) - backward_sum(partial_value, share_rows)
            ).astype(jnp.bfloat16)
        pieces.append(apply_inverse(inverse_diag[level_at, 0, 0], residual, True))
        bwd_levels[level_at] = pieces
    forward_rows = []
    backward_rows = []
    for level_at in range(levels):
        forward_rows.append(jnp.concatenate(fwd_levels[level_at], axis=1))
        backward_rows.append(jnp.concatenate(bwd_levels[level_at], axis=1))
    forward_solution = jnp.stack(forward_rows).reshape(levels, 1, 1, share_rows, rhs_cols)
    solution = jnp.stack(backward_rows).reshape(levels, 1, 1, share_rows, rhs_cols)
    return (forward_solution, solution)


def solution(mesh):
    placed = (
        P(None, "row", ("depth", "col"), None, None),
        P(None, "row", ("depth", "col"), None, None, None),
        P(None, "row", None, ("depth", "col"), None),
        P(None, "row", None, ("depth", "col"), None),
    )
    return jax.shard_map(
        body,
        mesh=mesh,
        in_specs=placed,
        out_specs=(
            P(None, "row", ("depth", "col"), None, None),
            P(None, "row", ("depth", "col"), None, None),
        ),
        check_vma=False,
    )
```

profile of v0, /device:TPU:0, one launch (start us, length us, event | category | flops | bytes accessed | tf_op | source)
XLA Modules:
  0.0 735.9 jit_solution(18099699853977080136)
XLA Ops:
  7.2 1.8 convolution_convert_fusion.10
  9.8 2.6 mul.62
  12.3 7.3 mul.63
  19.6 2.6 mul.71
  22.2 7.3 mul.72
  29.6 2.6 mul.67
  32.2 7.4 mul.68
  39.5 13.6 %slice_multiply_fusion.2 = (bf16[1,1,1024,1,2048]{4,2,3,1,0:T(8,128)(2,1)}, bf16[1,1,1024,1,2048]{4,2,3,1,0:T(8,128)(2,1)}, bf16[1,1,1024,1,2048]{4,2,3,1,0:T(8,128)(2,1)}) fusion(bf16[1,1,1024,1,2048]{4,2,3,1,0:T(8,128)(2,1)} %mul.63, bf16[3,1,1024,1,2048]{4,2,3,1,0:T(8,128)(2,1)} %param.6, bf16[1,1,1024,1,2048]{4,2,3,1,0:T(8,128)(2,1)} %mul.72, ...), kind=kLoop, calls=%fused_computation.8 | loop fusion | flops 6291456 | bytes 37748736 | tf_op jit(solution)/shard_map/mul | solution.py:57
  53.1 5.1 all-gather.13.cloned.1.call-done
  58.2 6.2 fusion.9
  64.5 62.1 %all-reduce.7.cloned.1.call-done = bf16[8,128,512]{2,1,0:T(8,128)(2,1)} async-done(((bf16[8,128,512]{2,1,0:T(8,128)(2,1)}), bf16[8,128,512]{2,1,0:T(8,128)(2,1)}) %all-reduce.7.cloned.1.call-update) | async-done | bytes 1048592 | tf_op jit(solution)/shard_map/psum | solution.py:37
  126.6 1.7 convolution_convert_fusion.5
  128.5 45.3 %all-gather.15.cloned.1.call-done = bf16[2048,512]{1,0:T(8,128)(2,1)} async-done(((bf16[128,512]{1,0:T(8,128)(2,1)}), bf16[2048,512]{1,0:T(8,128)(2,1)}) %all-gather.15.cloned.1.call-update) | async-done | bytes 2097168 | tf_op jit(solution)/shard_map/all_gather | solution.py:15
  173.7 6.2 fusion.12
  180.0 62.1 %all-reduce.9.cloned.1.call-done = bf16[8,128,512]{2,1,0:T(8,128)(2,1)} async-done(((bf16[8,128,512]{2,1,0:T(8,128)(2,1)}), bf16[8,128,512]{2,1,0:T(8,128)(2,1)}) %all-reduce.9.cloned.1.call-update) | async-done | bytes 1048592 | tf_op jit(solution)/shard_map/psum | solution.py:37
  243.9 44.5 %all-gather.17.cloned.1.call-done = bf16[2048,512]{1,0:T(8,128)(2,1)} async-done(((bf16[128,512]{1,0:T(8,128)(2,1)}), bf16[2048,512]{1,0:T(8,128)(2,1)}) %all-gather.17.cloned.1.call-update) | async-done | bytes 2097168 | tf_op jit(solution)/shard_map/all_gather | solution.py:15
  288.5 6.2 fusion.15
  294.7 62.1 %all-reduce.11.cloned.1.call-done = bf16[8,128,512]{2,1,0:T(8,128)(2,1)} async-done(((bf16[8,128,512]{2,1,0:T(8,128)(2,1)}), bf16[8,128,512]{2,1,0:T(8,128)(2,1)}) %all-reduce.11.cloned.1.call-update) | async-done | bytes 1048592 | tf_op jit(solution)/shard_map/psum | solution.py:37
  359.0 15.1 %fusion.2 = (bf16[2048,1024]{0,1:T(8,128)(2,1)}, bf16[2048,1024]{0,1:T(8,128)(2,1)}, bf16[2048,1024]{0,1:T(8,128)(2,1)}) fusion(bf16[128,8,16,128]{3,2,1,0:T(8,128)(2,1)} %bitcast.180, bf16[3,1,1024,1,2048]{4,2,3,1,0:T(8,128)(2,1)} %param.6, bf16[128,8,16,128]{3,2,1,0:T(8,128)(2,1)} %bitcast.182, bf16[128,8,16,128]{3,2,1,0:T(8,128)(2,1)} %bitcast.181), kind=kLoop, calls=%fused_computation.5 | loop fusion | flops 6291456 | bytes 37748736 | tf_op jit(solution)/shard_map/dot_general | solution.py:25
  374.1 6.4 copy.26
  381.6 6.3 convolution_convert_fusion.2
  387.9 92.3 %all-reduce.13.cloned.1.call-done = bf16[16,128,512]{2,1,0:T(8,128)(2,1)} async-done(((bf16[16,128,512]{2,1,0:T(8,128)(2,1)}), bf16[16,128,512]{2,1,0:T(8,128)(2,1)}) %all-reduce.13.cloned.1.call-update) | async-done | bytes 2097168 | tf_op jit(solution)/shard_map/psum | solution.py:43
  480.2 1.8 convolution_convert_fusion.8
  482.1 6.4 copy.25
  488.5 16.4 %all-gather.21.cloned.1.call-done = bf16[1024,512]{0,1:T(8,128)(2,1)} async-done(((bf16[128,512]{0,1:T(8,128)(2,1)}), bf16[1024,512]{0,1:T(8,128)(2,1)}) %all-gather.21.cloned.1.call-update) | async-done | bytes 1048592 | tf_op jit(solution)/shard_map/all_gather | solution.py:23
  504.9 6.3 convolution_convert_fusion.1
  511.2 92.3 %all-reduce.15.cloned.1.call-done = bf16[16,128,512]{2,1,0:T(8,128)(2,1)} async-done(((bf16[16,128,512]{2,1,0:T(8,128)(2,1)}), bf16[16,128,512]{2,1,0:T(8,128)(2,1)}) %all-reduce.15.cloned.1.call-update) | async-done | bytes 2097168 | tf_op jit(solution)/shard_map/psum | solution.py:43
  603.5 1.8 convolution_convert_fusion.7
  605.3 6.4 copy.24
  611.7 16.4 %all-gather.23.cloned.1.call-done = bf16[1024,512]{0,1:T(8,128)(2,1)} async-done(((bf16[128,512]{0,1:T(8,128)(2,1)}), bf16[1024,512]{0,1:T(8,128)(2,1)}) %all-gather.23.cloned.1.call-update) | async-done | bytes 1048592 | tf_op jit(solution)/shard_map/all_gather | solution.py:23
  628.2 6.3 convolution_convert_fusion
  635.3 91.5 %all-reduce.17.cloned.1.call-done = bf16[16,128,512]{2,1,0:T(8,128)(2,1)} async-done(((bf16[16,128,512]{2,1,0:T(8,128)(2,1)}), bf16[16,128,512]{2,1,0:T(8,128)(2,1)}) %all-reduce.17.cloned.1.call-update) | async-done | bytes 2097168 | tf_op jit(solution)/shard_map/psum | solution.py:43
  (50 shorter events, 9.4 us)
Async XLA Ops:
  7.2 51.1 %all-gather.13.cloned.1.call-start = ((), (), s32[]{:S(2)}) async-start(), calls=%async_computation.6 | async-start | bytes 2228224 | tf_op jit(solution)/shard_map/all_gather | solution.py:15
  9.0 117.6 %all-reduce.7.cloned.1.call-start = ((), (), s32[]{:S(2)}) async-start(), calls=%async_computation | async-start | bytes 2097152 | tf_op jit(solution)/shard_map/psum | solution.py:37
  58.2 68.4 %copy-start.6 = (bf16[4,1,1,128,512]{4,3,2,1,0:T(8,128)(2,1)S(1)}, bf16[4,1,1,128,512]{4,3,2,1,0:T(8,128)(2,1)}, u32[]{:S(2)}) copy-start(bf16[4,1,1,128,512]{4,3,2,1,0:T(8,128)(2,1)} %param.4) | copy-start | bytes 1572868
  58.2 68.4 %copy-start.7 = (bf16[4,1,1,1,128,128]{5,4,3,2,1,0:T(8,128)(2,1)S(1)}, bf16[4,1,1,1,128,128]{5,4,3,2,1,0:T(8,128)(2,1)}, u32[]{:S(2)}) copy-start(bf16[4,1,1,1,128,128]{5,4,3,2,1,0:T(8,128)(2,1)} %param.5) | copy-start | bytes 393220
  64.5 109.2 %all-gather.15.cloned.1.call-start = ((), (), s32[]{:S(2)}) async-start(), calls=%async_computation.7 | async-start | bytes 2228224 | tf_op jit(solution)/shard_map/all_gather | solution.py:15
  128.4 113.7 %all-reduce.9.cloned.1.call-start = ((), (), s32[]{:S(2)}) async-start(), calls=%async_computation.1 | async-start | bytes 2097152 | tf_op jit(solution)/shard_map/psum | solution.py:37
  180.0 108.5 %all-gather.17.cloned.1.call-start = ((), (), s32[]{:S(2)}) async-start(), calls=%async_computation.8 | async-start | bytes 2228224 | tf_op jit(solution)/shard_map/all_gather | solution.py:15
  243.9 113.0 %all-reduce.11.cloned.1.call-start = ((), (), s32[]{:S(2)}) async-start(), calls=%async_computation.2 | async-start | bytes 2097152 | tf_op jit(solution)/shard_map/psum | solution.py:37
  294.7 86.9 %all-gather.19.cloned.1.call-start = ((), (), s32[]{:S(2)}) async-start(), calls=%async_computation.9 | async-start | bytes 1179648 | tf_op jit(solution)/shard_map/all_gather | solution.py:23
  358.8 121.4 %all-reduce.13.cloned.1.call-start = ((), (), s32[]{:S(2)}) async-start(), calls=%async_computation.3 | async-start | bytes 4194304 | tf_op jit(solution)/shard_map/psum | solution.py:43
  381.6 98.7 %copy-start.2 = (bf16[512,128]{0,1:T(8,128)(2,1)S(1)}, bf16[512,128]{0,1:T(8,128)(2,1)}, u32[]{:S(2)}) copy-start(bf16[512,128]{0,1:T(8,128)(2,1)} %convolution_convert_fusion.4) | copy-start | bytes 393220
  387.9 117.0 %all-gather.21.cloned.1.call-start = ((), (), s32[]{:S(2)}) async-start(), calls=%async_computation.10 | async-start | bytes 1179648 | tf_op jit(solution)/shard_map/all_gather | solution.py:23
  482.0 121.4 %all-reduce.15.cloned.1.call-start = ((), (), s32[]{:S(2)}) async-start(), calls=%async_computation.4 | async-start | bytes 4194304 | tf_op jit(solution)/shard_map/psum | solution.py:43
  504.9 98.6 %copy-start.1 = (bf16[512,128]{0,1:T(8,128)(2,1)S(1)}, bf16[512,128]{0,1:T(8,128)(2,1)}, u32[]{:S(2)}) copy-start(bf16[512,128]{0,1:T(8,128)(2,1)} %convolution_convert_fusion.5) | copy-start | bytes 393220
  511.2 117.0 %all-gather.23.cloned.1.call-start = ((), (), s32[]{:S(2)}) async-start(), calls=%async_computation.11 | async-start | bytes 1179648 | tf_op jit(solution)/shard_map/all_gather | solution.py:23
  605.3 121.5 %all-reduce.17.cloned.1.call-start = ((), (), s32[]{:S(2)}) async-start(), calls=%async_computation.5 | async-start | bytes 4194304 | tf_op jit(solution)/shard_map/psum | solution.py:43
  628.1 6.3 copy-start
  628.1 99.8 %copy-start.3 = (bf16[512,128]{1,0:T(8,128)(2,1)S(1)}, bf16[512,128]{1,0:T(8,128)(2,1)}, u32[]{:S(2)}) copy-start(bf16[512,128]{1,0:T(8,128)(2,1)} %convolution_convert_fusion.9) | copy-start | bytes 393220
  628.1 99.8 %copy-start.4 = (bf16[512,128]{1,0:T(8,128)(2,1)S(1)}, bf16[512,128]{1,0:T(8,128)(2,1)}, u32[]{:S(2)}) copy-start(bf16[512,128]{1,0:T(8,128)(2,1)} %convolution_convert_fusion.8) | copy-start | bytes 393220
  628.2 99.8 %copy-start.5 = (bf16[512,128]{1,0:T(8,128)(2,1)S(1)}, bf16[512,128]{1,0:T(8,128)(2,1)}, u32[]{:S(2)}) copy-start(bf16[512,128]{1,0:T(8,128)(2,1)} %convolution_convert_fusion.7) | copy-start | bytes 393220
Sparse Core Ops, SparseCore 0:
  10.7 47.4 all-gather.12
  64.6 61.9 all-reduce.6
  129.4 44.3 all-gather.14
  180.1 61.9 all-reduce.8
  244.1 44.3 all-gather.16
  294.8 61.9 all-reduce.10
  358.9 22.6 all-gather.18
  388.0 92.1 all-reduce.12
  482.2 22.6 all-gather.20
  511.3 92.1 all-reduce.14
  605.4 22.6 all-gather.22
  634.6 92.1 all-reduce.16
where the time goes:
time: 737 us; the launch traced here: 736 us
  waiting for transfers between devices  591 us (80%)
  local copies, waits for them, and re-layouts  50 us (7%)
  matrix products  49.3 us (7%)
  other arithmetic  30.3 us (4%)
  between operations  14.3 us (2%)
    psum x3, waiting for transfers between devices, backward_sum(): summed = lax.psum(blocks.astype(jnp.bfloat16), 'row').astype(jnp.float32)  276 us
    psum x3, waiting for transfers between devices, forward_sum(): lax.psum(blocks.astype(jnp.bfloat16), ('depth', 'col')).astype(jnp.float32)  186 us
    all_gather x3, waiting for transfers between devices, lift_upward(): portion = lax.all_gather(share_in, 'row', axis=0, tiled=True)  94.9 us
    all_gather x3, waiting for transfers between devices, carry_downward(): portion = lax.all_gather(share_in, ('depth', 'col'), axis=1, tiled=True)  33.9 us
    mul x6, local copies, waits for them, and re-layouts, body(): slab.reshape(gate.shape[0], block_width, gate.shape[1], block_width)  29.7 us
    dot_general x3, local copies, waits for them, and re-layouts, carry_downward(): lax.dot_general(masked, portion.reshape(span_rows, portion.shape[-1]), ((...  19.2 us
    dot_general x3, matrix products, carry_downward(): lax.dot_general(masked, portion.reshape(span_rows, portion.shape[-1]), ((...  18.8 us
    dot_general x3, matrix products, lift_upward(): jnp.dot(masked, portion.reshape(span_rows, portion.shape[-1]), preferred_...  18.6 us
  transfers between devices with their start and end apart: 12, of which 12 were waited for; matrix products, arithmetic and copies ran while one was open for 11% of the time, Pallas kernels for 0%

commit v1 on v0

--- a/solution.py
+++ b/solution.py
@@ -12,7 +12,10 @@
 
 
 def lift_upward(masked, share_in):
-    portion = lax.all_gather(share_in, "row", axis=0, tiled=True)
+    series = []
+    for _ in range(lax.axis_size("row")):
+        series.append(share_in)
+    portion = jnp.concatenate(lax.all_to_all(jnp.stack(series, 0), "row", 0, 0), 0)
     span_rows = portion.shape[0] * portion.shape[2]
     return jnp.dot(
         masked, portion.reshape(span_rows, portion.shape[-1]), preferred_element_type=jnp.float32

time: 737 us -> 710 us (0.963)
  waiting for transfers between devices: 591 us -> 497 us
  blocking collectives: 0 us -> 66.6 us
  matrix products: 49.3 us -> 41.2 us
  starting transfers between devices: 0.68 us -> 8.55 us
    all_gather x3 -> x0, waiting for transfers between devices: 94.9 us -> none  [lift_upward(): portion = lax.all_gather(share_in, 'row', axis=0, tiled=True)]
    all_to_all x0 -> x2, blocking collectives: none -> 66.6 us  [lift_upward(): lax.all_to_all(jnp.stack(series, 0), 'row', 0, 0)]
    all_to_all x0 -> x1, starting transfers between devices: none -> 7.99 us  [lift_upward(): lax.all_to_all(jnp.stack(series, 0), 'row', 0, 0)]
  transfers between devices with their start and end apart: 12 -> 10, of which waited for: 12 -> 9; matrix products, arithmetic and copies ran while one was open for 11% -> 11% of each run, Pallas kernels for 0% -> 0%
where the time goes in v1:
time: 710 us; the launch traced here: 709 us
  waiting for transfers between devices  497 us (70%)
  blocking collectives  66.6 us (9%)
  local copies, waits for them, and re-layouts  51.9 us (7%)
  matrix products  41.2 us (6%)
  other arithmetic  29.3 us (4%)
  between operations  14 us (2%)
  starting transfers between devices  8.55 us (1%)
    psum x3, waiting for transfers between devices, backward_sum(): summed = lax.psum(blocks.astype(jnp.bfloat16), 'row').astype(jnp.float32)  276 us
    psum x3, waiting for transfers between devices, forward_sum(): lax.psum(blocks.astype(jnp.bfloat16), ('depth', 'col')).astype(jnp.float32)  187 us
    all_to_all x2, blocking collectives, lift_upward(): lax.all_to_all(jnp.stack(series, 0), 'row', 0, 0)  66.6 us
    all_gather x3, waiting for transfers between devices, carry_downward(): portion = lax.all_gather(share_in, ('depth', 'col'), axis=1, tiled=True)  33.9 us
    mul x6, local copies, waits for them, and re-layouts, body(): slab.reshape(gate.shape[0], block_width, gate.shape[1], block_width)  29.6 us
    dot_general x3, local copies, waits for them, and re-layouts, carry_downward(): lax.dot_general(masked, portion.reshape(span_rows, portion.shape[-1]), ((...  19.2 us
    dot_general x3, matrix products, carry_downward(): lax.dot_general(masked, portion.reshape(span_rows, portion.shape[-1]), ((...  18.7 us
    dot_general x1, other arithmetic, carry_downward(): lax.dot_general(masked, portion.reshape(span_rows, portion.shape[-1]), ((...  15.1 us
  transfers between devices with their start and end apart: 10, of which 9 were waited for; matrix products, arithmetic and copies ran while one was open for 11% of the time, Pallas kernels for 0%

profile of v1, /device:TPU:0, one launch (start us, length us, event | category | flops | bytes accessed | tf_op | source)
XLA Modules:
  0.0 708.6 jit_solution(9963009346857900268)
XLA Ops:
  8.3 1.6 stack.15
  9.9 8.0 %all-to-all-start = ((bf16[16,1,1,128,512]{4,3,2,1,0:T(8,128)(2,1)}), bf16[16,1,1,128,512]{4,3,2,1,0:T(8,128)(2,1)S(1)}, u32[]{:S(2)}, u32[]{:S(2)}) async-start(bf16[16,1,1,128,512]{4,3,2,1,0:T(8,128)(2,1)} %stack.15), calls=%async_computation | async-start | bytes 4194304 | tf_op jit(solution)/shard_map/all_to_all | solution.py:18
  17.9 2.5 mul.62
  20.5 7.3 %mul.63 = bf16[1,1,1024,1,2048]{4,2,3,1,0:T(8,128)(2,1)} reshape(bf16[8,128,16,128]{3,2,1,0:T(8,128)(2,1)} %mul.62) | data formatting | bytes 8388608 | tf_op jit(solution)/shard_map/mul | solution.py:60
  27.8 2.6 mul.71
  30.4 7.3 %mul.72 = bf16[1,1,1024,1,2048]{4,2,3,1,0:T(8,128)(2,1)} reshape(bf16[8,128,16,128]{3,2,1,0:T(8,128)(2,1)} %mul.71) | data formatting | bytes 8388608 | tf_op jit(solution)/shard_map/mul | solution.py:60
  37.7 2.6 mul.67
  40.3 7.3 %mul.68 = bf16[1,1,1024,1,2048]{4,2,3,1,0:T(8,128)(2,1)} reshape(bf16[8,128,16,128]{3,2,1,0:T(8,128)(2,1)} %mul.67) | data formatting | bytes 8388608 | tf_op jit(solution)/shard_map/mul | solution.py:60
  47.6 13.3 %slice_multiply_fusion.2 = (bf16[1,1,1024,1,2048]{4,2,3,1,0:T(8,128)(2,1)}, bf16[1,1,1024,1,2048]{4,2,3,1,0:T(8,128)(2,1)}, bf16[1,1,1024,1,2048]{4,2,3,1,0:T(8,128)(2,1)}) fusion(bf16[1,1,1024,1,2048]{4,2,3,1,0:T(8,128)(2,1)} %mul.63, bf16[3,1,1024,1,2048]{4,2,3,1,0:T(8,128)(2,1)} %param.6, bf16[1,1,1024,1,2048]{4,2,3,1,0:T(8,128)(2,1)} %mul.72, ...), kind=kLoop, calls=%fused_computation.8 | loop fusion | flops 6291456 | bytes 37748736 | tf_op jit(solution)/shard_map/mul | solution.py:60
  60.9 5.6 convolution_convert_fusion.5
  66.6 64.5 %all-reduce.7.cloned.1.call-done = bf16[8,128,512]{2,1,0:T(8,128)(2,1)} async-done(((bf16[8,128,512]{2,1,0:T(8,128)(2,1)}), bf16[8,128,512]{2,1,0:T(8,128)(2,1)}) %all-reduce.7.cloned.1.call-update) | async-done | bytes 1048592 | tf_op jit(solution)/shard_map/psum | solution.py:40
  131.1 1.2 convolution_convert_fusion.8
  132.6 33.3 %all_to_all.15 = bf16[16,1,1,128,512]{4,3,2,1,0:T(8,128)(2,1)S(1)} all-to-all(bf16[16,1,1,128,512]{4,3,2,1,0:T(8,128)(2,1)S(1)} %stack.16), channel_id=1, replica_groups=mesh['depth'=2,'row'=16,'col'=4] {'row'}, dimensions={0} | all-to-all | bytes 4194304 | tf_op jit(solution)/shard_map/all_to_all | solution.py:18
  165.9 3.3 convolution_convert_fusion.4
  169.3 61.3 %all-reduce.9.cloned.1.call-done = bf16[8,128,512]{2,1,0:T(8,128)(2,1)} async-done(((bf16[8,128,512]{2,1,0:T(8,128)(2,1)}), bf16[8,128,512]{2,1,0:T(8,128)(2,1)}) %all-reduce.9.cloned.1.call-update) | async-done | bytes 1048592 | tf_op jit(solution)/shard_map/psum | solution.py:40
  232.0 33.3 %all_to_all.16 = bf16[16,1,1,128,512]{4,3,2,1,0:T(8,128)(2,1)S(1)} all-to-all(bf16[16,1,1,128,512]{4,3,2,1,0:T(8,128)(2,1)S(1)} %stack.17), channel_id=1, replica_groups=mesh['depth'=2,'row'=16,'col'=4] {'row'}, dimensions={0} | all-to-all | bytes 4194304 | tf_op jit(solution)/shard_map/all_to_all | solution.py:18
  265.3 3.3 convolution_convert_fusion.3
  268.7 61.2 %all-reduce.11.cloned.1.call-done = bf16[8,128,512]{2,1,0:T(8,128)(2,1)} async-done(((bf16[8,128,512]{2,1,0:T(8,128)(2,1)}), bf16[8,128,512]{2,1,0:T(8,128)(2,1)}) %all-reduce.11.cloned.1.call-update) | async-done | bytes 1048592 | tf_op jit(solution)/shard_map/psum | solution.py:40
  332.1 15.1 %fusion.2 = (bf16[2048,1024]{0,1:T(8,128)(2,1)}, bf16[2048,1024]{0,1:T(8,128)(2,1)}, bf16[2048,1024]{0,1:T(8,128)(2,1)}) fusion(bf16[128,8,16,128]{3,2,1,0:T(8,128)(2,1)} %bitcast.177, bf16[3,1,1024,1,2048]{4,2,3,1,0:T(8,128)(2,1)} %param.6, bf16[128,8,16,128]{3,2,1,0:T(8,128)(2,1)} %bitcast.179, bf16[128,8,16,128]{3,2,1,0:T(8,128)(2,1)} %bitcast.178), kind=kLoop, calls=%fused_computation.5 | loop fusion | flops 6291456 | bytes 37748736 | tf_op jit(solution)/shard_map/dot_general | solution.py:28
  347.2 6.4 copy.38
  354.7 6.2 convolution_convert_fusion.2
  361.0 92.3 %all-reduce.13.cloned.1.call-done = bf16[16,128,512]{2,1,0:T(8,128)(2,1)} async-done(((bf16[16,128,512]{2,1,0:T(8,128)(2,1)}), bf16[16,128,512]{2,1,0:T(8,128)(2,1)}) %all-reduce.13.cloned.1.call-update) | async-done | bytes 2097168 | tf_op jit(solution)/shard_map/psum | solution.py:46
  453.3 1.8 convolution_convert_fusion.11
  455.1 6.4 copy.37
  461.5 16.4 %all-gather.9.cloned.1.call-done = bf16[1024,512]{0,1:T(8,128)(2,1)} async-done(((bf16[128,512]{0,1:T(8,128)(2,1)}), bf16[1024,512]{0,1:T(8,128)(2,1)}) %all-gather.9.cloned.1.call-update) | async-done | bytes 1048592 | tf_op jit(solution)/shard_map/all_gather | solution.py:26
  477.9 6.2 convolution_convert_fusion.1
  484.2 92.3 %all-reduce.15.cloned.1.call-done = bf16[16,128,512]{2,1,0:T(8,128)(2,1)} async-done(((bf16[16,128,512]{2,1,0:T(8,128)(2,1)}), bf16[16,128,512]{2,1,0:T(8,128)(2,1)}) %all-reduce.15.cloned.1.call-update) | async-done | bytes 2097168 | tf_op jit(solution)/shard_map/psum | solution.py:46
  576.5 1.8 convolution_convert_fusion.10
  578.3 6.4 copy.36
  584.8 16.4 %all-gather.11.cloned.1.call-done = bf16[1024,512]{0,1:T(8,128)(2,1)} async-done(((bf16[128,512]{0,1:T(8,128)(2,1)}), bf16[1024,512]{0,1:T(8,128)(2,1)}) %all-gather.11.cloned.1.call-update) | async-done | bytes 1048592 | tf_op jit(solution)/shard_map/all_gather | solution.py:26
  601.2 6.3 convolution_convert_fusion
  608.3 91.5 %all-reduce.17.cloned.1.call-done = bf16[16,128,512]{2,1,0:T(8,128)(2,1)} async-done(((bf16[16,128,512]{2,1,0:T(8,128)(2,1)}), bf16[16,128,512]{2,1,0:T(8,128)(2,1)}) %all-reduce.17.cloned.1.call-update) | async-done | bytes 2097168 | tf_op jit(solution)/shard_map/psum | solution.py:46
  (48 shorter events, 9.6 us)
Async XLA Ops:
  7.2 10.8 %copy-start.7 = (s32[3,1,8,1,16]{4,3,2,1,0:T(1,128)S(1)}, s32[3,1,8,1,16]{4,3,2,1,0:T(1,128)}, u32[]{:S(2)}) copy-start(s32[3,1,8,1,16]{4,3,2,1,0:T(1,128)} %param.7) | copy-start | bytes 4612
  9.9 51.0 %all-to-all-start = ((bf16[16,1,1,128,512]{4,3,2,1,0:T(8,128)(2,1)}), bf16[16,1,1,128,512]{4,3,2,1,0:T(8,128)(2,1)S(1)}, u32[]{:S(2)}, u32[]{:S(2)}) async-start(bf16[16,1,1,128,512]{4,3,2,1,0:T(8,128)(2,1)} %stack.15), calls=%async_computation | async-start | bytes 4194304 | tf_op jit(solution)/shard_map/all_to_all | solution.py:18
  17.9 113.2 %all-reduce.7.cloned.1.call-start = ((), (), s32[]{:S(2)}) async-start(), calls=%async_computation.3 | async-start | bytes 2097152 | tf_op jit(solution)/shard_map/psum | solution.py:40
  60.9 70.2 %copy-start.5 = (bf16[4,1,1,128,512]{4,3,2,1,0:T(8,128)(2,1)S(1)}, bf16[4,1,1,128,512]{4,3,2,1,0:T(8,128)(2,1)}, u32[]{:S(2)}) copy-start(bf16[4,1,1,128,512]{4,3,2,1,0:T(8,128)(2,1)} %param.4) | copy-start | bytes 1572868
  60.9 70.2 %copy-start.6 = (bf16[4,1,1,1,128,128]{5,4,3,2,1,0:T(8,128)(2,1)S(1)}, bf16[4,1,1,1,128,128]{5,4,3,2,1,0:T(8,128)(2,1)}, u32[]{:S(2)}) copy-start(bf16[4,1,1,1,128,128]{5,4,3,2,1,0:T(8,128)(2,1)} %param.5) | copy-start | bytes 393220
  66.6 164.0 %all-reduce.9.cloned.1.call-start = ((), (), s32[]{:S(2)}) async-start(), calls=%async_computation.4 | async-start | bytes 2097152 | tf_op jit(solution)/shard_map/psum | solution.py:40
  131.1 34.8 %copy-start.1 = (bf16[1,1,1024,1,2048]{4,2,3,1,0:T(8,128)(2,1)S(1)}, bf16[1,1,1024,1,2048]{4,2,3,1,0:T(8,128)(2,1)}, u32[]{:S(2)}) copy-start(bf16[1,1,1024,1,2048]{4,2,3,1,0:T(8,128)(2,1)} %get-tuple-element.11) | copy-start | bytes 12582916
  169.2 160.7 %all-reduce.11.cloned.1.call-start = ((), (), s32[]{:S(2)}) async-start(), calls=%async_computation.5 | async-start | bytes 2097152 | tf_op jit(solution)/shard_map/psum | solution.py:40
  230.6 34.8 %copy-start = (bf16[1,1,1024,1,2048]{4,2,3,1,0:T(8,128)(2,1)S(1)}, bf16[1,1,1024,1,2048]{4,2,3,1,0:T(8,128)(2,1)}, u32[]{:S(2)}) copy-start(bf16[1,1,1024,1,2048]{4,2,3,1,0:T(8,128)(2,1)} %get-tuple-element.10) | copy-start | bytes 12582916
  268.7 86.0 %all-gather.7.cloned.1.call-start = ((), (), s32[]{:S(2)}) async-start(), calls=%async_computation.9 | async-start | bytes 1179648 | tf_op jit(solution)/shard_map/all_gather | solution.py:26
  331.9 121.4 %all-reduce.13.cloned.1.call-start = ((), (), s32[]{:S(2)}) async-start(), calls=%async_computation.6 | async-start | bytes 4194304 | tf_op jit(solution)/shard_map/psum | solution.py:46
  360.9 117.0 %all-gather.9.cloned.1.call-start = ((), (), s32[]{:S(2)}) async-start(), calls=%async_computation.10 | async-start | bytes 1179648 | tf_op jit(solution)/shard_map/all_gather | solution.py:26
  455.1 121.5 %all-reduce.15.cloned.1.call-start = ((), (), s32[]{:S(2)}) async-start(), calls=%async_computation.7 | async-start | bytes 4194304 | tf_op jit(solution)/shard_map/psum | solution.py:46
  484.2 117.0 %all-gather.11.cloned.1.call-start = ((), (), s32[]{:S(2)}) async-start(), calls=%async_computation.11 | async-start | bytes 1179648 | tf_op jit(solution)/shard_map/all_gather | solution.py:26
  578.3 121.5 %all-reduce.17.cloned.1.call-start = ((), (), s32[]{:S(2)}) async-start(), calls=%async_computation.8 | async-start | bytes 4194304 | tf_op jit(solution)/shard_map/psum | solution.py:46
  601.2 99.8 %copy-start.2 = (bf16[512,128]{1,0:T(8,128)(2,1)S(1)}, bf16[512,128]{1,0:T(8,128)(2,1)}, u32[]{:S(2)}) copy-start(bf16[512,128]{1,0:T(8,128)(2,1)} %convolution_convert_fusion.12) | copy-start | bytes 393220
  601.2 99.8 %copy-start.3 = (bf16[512,128]{1,0:T(8,128)(2,1)S(1)}, bf16[512,128]{1,0:T(8,128)(2,1)}, u32[]{:S(2)}) copy-start(bf16[512,128]{1,0:T(8,128)(2,1)} %convolution_convert_fusion.11) | copy-start | bytes 393220
  601.2 99.8 %copy-start.4 = (bf16[512,128]{1,0:T(8,128)(2,1)S(1)}, bf16[512,128]{1,0:T(8,128)(2,1)}, u32[]{:S(2)}) copy-start(bf16[512,128]{1,0:T(8,128)(2,1)} %convolution_convert_fusion.10) | copy-start | bytes 393220
Sparse Core Ops, SparseCore 0:
  66.7 64.3 all-reduce.6
  169.3 61.1 all-reduce.8
  268.8 61.0 all-reduce.10
  332.0 22.6 all-gather.6
  361.0 92.1 all-reduce.12
  455.2 22.6 all-gather.8
  484.3 92.1 all-reduce.14
  578.4 22.6 all-gather.10
  607.6 92.2 all-reduce.16
